TPU v7x, 32 devices: a whole 2x2x4 slice. The times are simulated.
32 devices in a mesh: dp: 8 (over z, x), vocab: 4 (over y, core).
Axes of the slice: x: 2, y: 2, z: 4, core: 2. Of those that a mesh axis runs over, the one named last changes fastest.
Arguments:
- hidden_states: bfloat16 [1024, 3584], P('dp', 'vocab'), may hold values from -750 to 750, as said below
- head_weight: bfloat16 [152064, 3584], P(('dp', 'vocab')), may hold values from -0.09375 to 0.09375
- token_ids: int32 [1024], P('dp'), may hold values from 0 to 152063
- response_mask: int32 [1024], P('dp'), may hold values 0 or 1
- rollout_logprobs: float32 [1024], P('dp'), may hold values from -14 to -6
- advantages: float32 [1024], P('dp'), may hold values from -6 to 6
Outputs:
- logprobs: float32 [1024], P('dp')
- tis_weight: float32 [1024], P('dp')
- loss: float32 [], replicated
Inputs may be any that keep to these rules, and one draw needn't show every extreme that they name: `hidden_states`: hidden states; some rows may be far larger than others.
All inputs are finite; a program needn't handle non-finite values. No bound on the sum of `response_mask` on one device may be relied on, other than what follows from the above.
Results may differ from a plain program's by a relative error of at most 0.0003.
Values may be sent and summed in bfloat16 or wider, within the bound.
A program may use at most 128 MiB of HBM per device.

v0:
```python
import jax
import jax.numpy as jnp
from jax import lax
from jax.sharding import PartitionSpec as P


def shard_stats(logits, ids_block, columns):
    matched = columns[None, :] == ids_block[:, None]
    picked = jnp.sum(jnp.where(matched, logits, 0.0), axis=1)
    peak = jnp.max(logits, axis=1)
    total = jnp.sum(jnp.exp(logits - peak[:, None]), axis=1)
    return (peak, total, picked)


def token_terms(logp, rollout, advant, mask):
    weight = jnp.minimum(jnp.exp(logp - rollout), 2.0)
    counted = mask.astype(jnp.float32)
    loss_part = -jnp.sum(counted * weight * advant * logp)
    return (weight, loss_part, jnp.sum(counted))


def body(hidden_states, head_weight, token_ids, response_mask, rollout_logprobs, advantages):
    rows_local = token_ids.shape[0]
    vocab_local = head_weight.shape[0]
    offset = lax.axis_index(("dp", "vocab")) * vocab_local
    own_columns = lax.iota(jnp.int32, vocab_local) + offset
    dp_index = lax.axis_index("dp")
    own_start = dp_index * rows_local
    all_ids, all_mask = (
        lax.all_gather(token_ids, "dp", axis=0, tiled=True),
        lax.all_gather(response_mask, "dp", axis=0, tiled=True),
    )
    all_rollout, all_advant = (
        lax.all_gather(rollout_logprobs, "dp", axis=0, tiled=True),
        lax.all_gather(advantages, "dp", axis=0, tiled=True),
    )
    full_rows = lax.all_gather(hidden_states, "vocab", axis=1, tiled=True)
    logits = jnp.einsum(
        "rd,vd->rv",
        lax.all_gather(full_rows, "dp", axis=0, tiled=True),
        head_weight,
        preferred_element_type=jnp.float32,
    )
    peak, total, picked = shard_stats(logits, all_ids, own_columns)
    peak, total, picked = (peak, total, picked)
    top = lax.pmax(peak, ("dp", "vocab"))
    total_sum, picked_sum = lax.psum((total * jnp.exp(peak - top), picked), ("dp", "vocab"))
    logprob_all = picked_sum - (top + jnp.log(total_sum))
    own_logp = lax.dynamic_slice_in_dim(logprob_all, own_start, rows_local, 0)
    weight_all, loss_sum, count = token_terms(logprob_all, all_rollout, all_advant, all_mask)
    weight = lax.dynamic_slice_in_dim(weight_all, own_start, rows_local, 0)
    loss = loss_sum / jnp.maximum(count, 1.0)
    return (own_logp, weight, loss)


def solution(mesh):
    placed = (P("dp", "vocab"), P(("dp", "vocab"), None), P("dp"), P("dp"), P("dp"), P("dp"))
    return jax.shard_map(
        body, mesh=mesh, in_specs=placed, out_specs=(P("dp"), P("dp"), P()), check_vma=False
    )
```

profile of v0, /device:TPU:0, one launch (start us, length us, event | category | flops | bytes accessed | tf_op | source)
XLA Modules:
  0.0 274.0 jit_solution(17611963197525337187)
XLA Ops:
  7.2 0.0 all-gather.6.cloned.1.call-start
  7.2 12.5 %all_gather.19 = bf16[128,3584]{1,0:T(8,128)(2,1)} all-gather(bf16[128,896]{1,0:T(8,128)(2,1)} %param.6), channel_id=1, replica_groups=mesh['dp'=8,'vocab'=4] {'vocab'}, dimensions={1}, use_global_device_ids=true | all-gather | bytes 1146880 | tf_op jit(solution)/shard_map/all_gather | solution.py:37
  19.7 0.0 all-gather.6.cloned.1.call-update
  19.7 21.4 %all-gather.2 = s32[8,1,128]{2,1,0:T(1,128)S(1)} all-gather(s32[1,1,128]{2,1,0:T(1,128)} %bitcast.15), channel_id=1, replica_groups=mesh['dp'=8,'vocab'=4] {'dp'}, dimensions={0}, use_global_device_ids=true | all-gather | bytes 4608 | tf_op jit(solution)/shard_map/all_gather | solution.py:31
  41.2 0.6 convert_reduce_fusion
  42.4 17.1 %all-gather = s32[8,1,128]{2,1,0:T(1,128)S(1)} all-gather(s32[1,1,128]{2,1,0:T(1,128)} %bitcast.16), channel_id=1, replica_groups=mesh['dp'=8,'vocab'=4] {'dp'}, dimensions={0}, use_global_device_ids=true | all-gather | bytes 4608 | tf_op jit(solution)/shard_map/all_gather | solution.py:30
  59.5 18.8 %all-gather.1 = f32[8,1,128]{2,1,0:T(1,128)S(1)} all-gather(f32[1,1,128]{2,1,0:T(1,128)} %bitcast.17), channel_id=1, replica_groups=mesh['dp'=8,'vocab'=4] {'dp'}, dimensions={0}, use_global_device_ids=true | all-gather | bytes 4608 | tf_op jit(solution)/shard_map/all_gather | solution.py:34
  78.3 17.3 %all-gather.3 = f32[8,1,128]{2,1,0:T(1,128)S(1)} all-gather(f32[1,1,128]{2,1,0:T(1,128)} %bitcast.18), channel_id=1, replica_groups=mesh['dp'=8,'vocab'=4] {'dp'}, dimensions={0}, use_global_device_ids=true | all-gather | bytes 4608 | tf_op jit(solution)/shard_map/all_gather | solution.py:35
  95.6 36.2 %all-gather.6.cloned.1.call-done = bf16[1024,3584]{1,0:T(8,128)(2,1)} async-done(((bf16[128,3584]{1,0:T(8,128)(2,1)}), bf16[1024,3584]{1,0:T(8,128)(2,1)}) %all-gather.6.cloned.1.call-update) | async-done | bytes 7340048 | tf_op jit(solution)/shard_map/all_gather | solution.py:40
  131.8 43.0 %fusion = (f32[1024]{0:T(1024)S(1)}, f32[1024,4752]{0,1:T(8,128)}) fusion(bf16[1024,3584]{1,0:T(8,128)(2,1)} %all-gather.6.cloned.1.call-done, bf16[4752,3584]{1,0:T(8,128)(2,1)} %param.7), kind=kOutput, calls=%fused_computation.8 | convolution fusion | flops 34884698112 | bytes 60870656 | tf_op jit(solution)/shard_map/rd,vd->rv/dot_general | solution.py:38
  174.8 38.4 %pmax.7 = f32[1024]{0:T(1024)S(1)} all-reduce(f32[1024]{0:T(1024)S(1)} %get-tuple-element.9), channel_id=1, replica_groups=mesh['dp'=8,'vocab'=4] {'dp','vocab'}, use_global_device_ids=true, to_apply=%region_3.4 | all-reduce | flops 1024 | bytes 8192 | tf_op jit(solution)/shard_map/pmax | solution.py:46
  213.1 9.5 %exponential_reduce_fusion = (f32[1024]{0:T(1024)S(1)}, f32[1024]{0:T(1024)S(1)}) fusion(f32[1024,4752]{0,1:T(8,128)} %get-tuple-element.10, f32[1024]{0:T(1024)S(1)} %get-tuple-element.9, s32[1024]{0:T(1024)S(1)} %bitcast.14, s32[4752]{0:T(1024)S(1)} %iota_add_fusion), kind=kLoop, calls=%fused_computation | loop fusion | flops 24328192 | bytes 19499584 | tf_op jit(solution)/shard_map/reduce_sum | solution.py:11
  222.7 40.8 %all-reduce = (f32[1024]{0:T(1024)S(1)}, f32[1024]{0:T(1024)S(1)}) all-reduce(f32[1024]{0:T(1024)S(1)} %get-tuple-element.4, f32[1024]{0:T(1024)S(1)} %exponential_multiply_fusion), channel_id=1, replica_groups=mesh['dp'=8,'vocab'=4] {'dp','vocab'}, use_global_device_ids=true, to_apply=%region_1.2 | all-reduce | flops 2048 | bytes 16384 | tf_op jit(solution)/shard_map/psum | solution.py:47
  263.5 0.6 multiply_reduce_fusion
  264.1 0.6 dynamic_slice.6
  264.7 0.6 dynamic_slice.7
  (4 shorter events, 0.0 us)
Async XLA Ops:
  7.2 124.6 %all-gather.6.cloned.1.call-start = ((), (), s32[]{:S(2)}) async-start(), calls=%async_computation | async-start | bytes 8257536 | tf_op jit(solution)/shard_map/all_gather | solution.py:40
Sparse Core Ops, SparseCore 0:
  19.8 111.9 all-gather.5
where the time goes:
time: 275 us; the launch traced here: 274 us
  blocking collectives  166 us (60%)
  matrix products  43 us (16%)
  waiting for transfers between devices  36.2 us (13%)
  between operations  16.5 us (6%)
  other arithmetic  10.8 us (4%)
    dot_general x1, matrix products, body(): jnp.einsum('rd,vd->rv', lax.all_gather(full_rows, 'dp', axis=0, tiled=Tru...  43 us
    psum x1, blocking collectives, body(): lax.psum((total * jnp.exp(peak - top), picked), ('dp', 'vocab'))  40.8 us
    pmax x1, blocking collectives, body(): top = lax.pmax(peak, ('dp', 'vocab'))  38.4 us
    all_gather x1, waiting for transfers between devices, body(): lax.all_gather(full_rows, 'dp', axis=0, tiled=True)  36.2 us
    all_gather x1, blocking collectives, body(): lax.all_gather(response_mask, 'dp', axis=0, tiled=True)  21.4 us
    all_gather x1, blocking collectives, body(): lax.all_gather(rollout_logprobs, 'dp', axis=0, tiled=True)  18.8 us
    all_gather x1, blocking collectives, body(): lax.all_gather(advantages, 'dp', axis=0, tiled=True)  17.3 us
    all_gather x1, blocking collectives, body(): lax.all_gather(token_ids, 'dp', axis=0, tiled=True)  17.1 us
  transfers between devices with their start and end apart: 1, of which 1 were waited for; matrix products, arithmetic and copies ran while one was open for 0% of the time, Pallas kernels for 0%

commit v1 on v0

--- a/solution.py
+++ b/solution.py
@@ -44,7 +44,7 @@
     peak, total, picked = shard_stats(logits, all_ids, own_columns)
     peak, total, picked = (peak, total, picked)
     top = lax.pmax(peak, ("dp", "vocab"))
-    total_sum, picked_sum = lax.psum((total * jnp.exp(peak - top), picked), ("dp", "vocab"))
+    total_sum, picked_sum = lax.psum(lax.psum((total * jnp.exp(peak - top), picked), "vocab"), "dp")
     logprob_all = picked_sum - (top + jnp.log(total_sum))
     own_logp = lax.dynamic_slice_in_dim(logprob_all, own_start, rows_local, 0)
     weight_all, loss_sum, count = token_terms(logprob_all, all_rollout, all_advant, all_mask)

time: 275 us -> 261 us (0.949)
  blocking collectives: 166 us -> 153 us
    psum x1 -> x2, blocking collectives: 40.8 us -> 27.1 us  [the longest x1 20.5 us: body(): lax.psum(lax.psum((total * jnp.exp(peak - top), picked), 'vocab'), 'dp')]
where the time goes in v1:
time: 261 us; the launch traced here: 260 us
  blocking collectives  153 us (59%)
  matrix products  43 us (16%)
  waiting for transfers between devices  36.2 us (14%)
  between operations  16.5 us (6%)
  other arithmetic  10.8 us (4%)
    dot_general x1, matrix products, body(): jnp.einsum('rd,vd->rv', lax.all_gather(full_rows, 'dp', axis=0, tiled=Tru...  43 us
    pmax x1, blocking collectives, body(): top = lax.pmax(peak, ('dp', 'vocab'))  38.3 us
    all_gather x1, waiting for transfers between devices, body(): lax.all_gather(full_rows, 'dp', axis=0, tiled=True)  36.2 us
    all_gather x1, blocking collectives, body(): lax.all_gather(response_mask, 'dp', axis=0, tiled=True)  21.4 us
    psum x1, blocking collectives, body(): lax.psum(lax.psum((total * jnp.exp(peak - top), picked), 'vocab'), 'dp')  20.5 us
    all_gather x1, blocking collectives, body(): lax.all_gather(rollout_logprobs, 'dp', axis=0, tiled=True)  18.8 us
    all_gather x1, blocking collectives, body(): lax.all_gather(advantages, 'dp', axis=0, tiled=True)  17.3 us
    all_gather x1, blocking collectives, body(): lax.all_gather(token_ids, 'dp', axis=0, tiled=True)  17.1 us
  transfers between devices with their start and end apart: 1, of which 1 were waited for; matrix products, arithmetic and copies ran while one was open for 0% of the time, Pallas kernels for 0%

profile of v1, /device:TPU:0, one launch (start us, length us, event | category | flops | bytes accessed | tf_op | source)
XLA Modules:
  0.0 260.3 jit_solution(4974173748120706496)
XLA Ops:
  7.2 0.0 all-gather.6.cloned.1.call-start
  7.2 12.5 %all_gather.19 = bf16[128,3584]{1,0:T(8,128)(2,1)} all-gather(bf16[128,896]{1,0:T(8,128)(2,1)} %param.6), channel_id=1, replica_groups=mesh['dp'=8,'vocab'=4] {'vocab'}, dimensions={1}, use_global_device_ids=true | all-gather | bytes 1146880 | tf_op jit(solution)/shard_map/all_gather | solution.py:37
  19.7 0.0 all-gather.6.cloned.1.call-update
  19.7 21.4 %all-gather.2 = s32[8,1,128]{2,1,0:T(1,128)S(1)} all-gather(s32[1,1,128]{2,1,0:T(1,128)} %bitcast.15), channel_id=1, replica_groups=mesh['dp'=8,'vocab'=4] {'dp'}, dimensions={0}, use_global_device_ids=true | all-gather | bytes 4608 | tf_op jit(solution)/shard_map/all_gather | solution.py:31
  41.2 0.6 convert_reduce_fusion
  42.4 17.1 %all-gather = s32[8,1,128]{2,1,0:T(1,128)S(1)} all-gather(s32[1,1,128]{2,1,0:T(1,128)} %bitcast.16), channel_id=1, replica_groups=mesh['dp'=8,'vocab'=4] {'dp'}, dimensions={0}, use_global_device_ids=true | all-gather | bytes 4608 | tf_op jit(solution)/shard_map/all_gather | solution.py:30
  59.5 18.8 %all-gather.1 = f32[8,1,128]{2,1,0:T(1,128)S(1)} all-gather(f32[1,1,128]{2,1,0:T(1,128)} %bitcast.17), channel_id=1, replica_groups=mesh['dp'=8,'vocab'=4] {'dp'}, dimensions={0}, use_global_device_ids=true | all-gather | bytes 4608 | tf_op jit(solution)/shard_map/all_gather | solution.py:34
  78.3 17.3 %all-gather.3 = f32[8,1,128]{2,1,0:T(1,128)S(1)} all-gather(f32[1,1,128]{2,1,0:T(1,128)} %bitcast.18), channel_id=1, replica_groups=mesh['dp'=8,'vocab'=4] {'dp'}, dimensions={0}, use_global_device_ids=true | all-gather | bytes 4608 | tf_op jit(solution)/shard_map/all_gather | solution.py:35
  95.6 36.2 %all-gather.6.cloned.1.call-done = bf16[1024,3584]{1,0:T(8,128)(2,1)} async-done(((bf16[128,3584]{1,0:T(8,128)(2,1)}), bf16[1024,3584]{1,0:T(8,128)(2,1)}) %all-gather.6.cloned.1.call-update) | async-done | bytes 7340048 | tf_op jit(solution)/shard_map/all_gather | solution.py:40
  131.8 43.0 %fusion = (f32[1024]{0:T(1024)S(1)}, f32[1024,4752]{0,1:T(8,128)}) fusion(bf16[1024,3584]{1,0:T(8,128)(2,1)} %all-gather.6.cloned.1.call-done, bf16[4752,3584]{1,0:T(8,128)(2,1)} %param.7), kind=kOutput, calls=%fused_computation.8 | convolution fusion | flops 34884698112 | bytes 60870656 | tf_op jit(solution)/shard_map/rd,vd->rv/dot_general | solution.py:38
  174.8 38.3 %pmax.7 = f32[1024]{0:T(1024)S(1)} all-reduce(f32[1024]{0:T(1024)S(1)} %get-tuple-element.11), channel_id=1, replica_groups=mesh['dp'=8,'vocab'=4] {'dp','vocab'}, use_global_device_ids=true, to_apply=%region_4.5 | all-reduce | flops 1024 | bytes 8192 | tf_op jit(solution)/shard_map/pmax | solution.py:46
  213.1 9.5 %exponential_reduce_fusion = (f32[1024]{0:T(1024)S(1)}, f32[1024]{0:T(1024)S(1)}) fusion(f32[1024,4752]{0,1:T(8,128)} %get-tuple-element.12, f32[1024]{0:T(1024)S(1)} %get-tuple-element.11, s32[1024]{0:T(1024)S(1)} %bitcast.14, s32[4752]{0:T(1024)S(1)} %iota_add_fusion), kind=kLoop, calls=%fused_computation | loop fusion | flops 24328192 | bytes 19499584 | tf_op jit(solution)/shard_map/reduce_sum | solution.py:11
  222.7 6.7 %all-reduce.1 = (f32[1024]{0:T(1024)S(1)}, f32[1024]{0:T(1024)S(1)}) all-reduce(f32[1024]{0:T(1024)S(1)} %get-tuple-element.4, f32[1024]{0:T(1024)S(1)} %exponential_multiply_fusion), channel_id=1, replica_groups=mesh['dp'=8,'vocab'=4] {'vocab'}, use_global_device_ids=true, to_apply=%region_1.2 | all-reduce | flops 2048 | bytes 16384 | tf_op jit(solution)/shard_map/psum | solution.py:47
  229.3 20.5 %all-reduce = (f32[1024]{0:T(1024)S(1)}, f32[1024]{0:T(1024)S(1)}) all-reduce(f32[1024]{0:T(1024)S(1)} %get-tuple-element.7, f32[1024]{0:T(1024)S(1)} %get-tuple-element.8), channel_id=1, replica_groups=mesh['dp'=8,'vocab'=4] {'dp'}, use_global_device_ids=true, to_apply=%region_2.3 | all-reduce | flops 2048 | bytes 16384 | tf_op jit(solution)/shard_map/psum | solution.py:47
  249.8 0.6 multiply_reduce_fusion
  250.4 0.6 dynamic_slice.6
  251.0 0.6 dynamic_slice.7
  (4 shorter events, 0.0 us)
Async XLA Ops:
  7.2 124.6 %all-gather.6.cloned.1.call-start = ((), (), s32[]{:S(2)}) async-start(), calls=%async_computation | async-start | bytes 8257536 | tf_op jit(solution)/shard_map/all_gather | solution.py:40
Sparse Core Ops, SparseCore 0:
  19.8 111.9 all-gather.5
